TPU v7x, 512 devices: a whole 4x8x8 slice. The times are simulated.
512 devices in a mesh: row: 32 (over y, z_lo), col: 16 (over z_hi, x, core).
Axes of the slice: x: 4, y: 8, z: 8 (z_hi: 2, z_lo: 4; z = z_hi * 4 + z_lo), core: 2. Of those that a mesh axis runs over, the one named last changes fastest.
Arguments:
- spectra: bfloat16 [4096, 16, 128], P(('row', 'col')), may hold values from -4 to 4
- window_flags: int32 [4096, 64], P(('row', 'col')), may hold values 0 or 1
- pair_mask: int32 [4096, 4096], P('row', 'col'), may hold values 0 or 1
- misfit_weight: bfloat16 [16, 4096, 4096], P(None, 'row', 'col'), may hold values from 0.0099487305 to 0.099609375
- observed: bfloat16 [2, 16, 4096, 4096], P(None, None, 'row', 'col'), may hold values from -6 to 6
Outputs:
- grad_first: bfloat16 [4096, 16, 128], P(('row', 'col'))
- grad_second: bfloat16 [16, 256, 16, 128], P('col', 'row')
All inputs are finite; a program needn't handle non-finite values. No bound on the sum of `window_flags` or of `pair_mask` on one device may be relied on, other than what follows from the above.
Results may differ from a plain program's by a relative error of at most 0.019.
Values may be sent and summed in bfloat16 or wider, within the bound.
A program may use at most 64 MiB of HBM per device.

v0:
```python
import jax
import jax.numpy as jnp
from jax import lax
from jax.sharding import PartitionSpec as P


def from_everyone(shard, axis):
    copies = jnp.broadcast_to(shard, (lax.axis_size(axis), *shard.shape))
    return lax.all_to_all(copies, axis, split_axis=0, concat_axis=0, tiled=True)


def in_order(blocks, dim):
    dims = list(blocks.shape[1:])
    dims[dim] *= blocks.shape[0]
    return jnp.moveaxis(blocks, 0, dim).reshape(dims)


def gather_directly(shard, axis, dim):
    blocks = from_everyone(shard, axis)
    return in_order(blocks, dim)


def split_up(shard, dim, count):
    before, after = (shard.shape[:dim], shard.shape[dim + 1 :])
    return jnp.moveaxis(shard.reshape(*before, count, -1, *after), dim, 0)


def summed_on_arrival(shard, axis, dim):
    blocks = split_up(shard, dim, lax.axis_size(axis))
    arrived = lax.all_to_all(blocks, axis, split_axis=0, concat_axis=0, tiled=True)
    return arrived.astype(jnp.float32).sum(axis=0)


def swap_parts(values, half_width):
    return jnp.concatenate([-values[..., half_width:], values[..., :half_width]], axis=-1)


def per_device(spectra, window_flags, pair_mask, misfit_weight, observed):
    half_width = spectra.shape[2] // 2
    flag_value = window_flags.astype(jnp.bfloat16)
    flag_both = jnp.concatenate([flag_value, flag_value], axis=1)
    flagged = spectra * flag_both[:, None, :]
    first_side = gather_directly(flagged, "col", 0)
    block_ratio = lax.axis_size("row") // lax.axis_size("col")
    strided = gather_directly(flagged, "row", 0)
    regrouped = lax.all_to_all(strided, "col", split_axis=0, concat_axis=0, tiled=True)
    col_count = lax.axis_size("col")
    shard_rows = flagged.shape[0]
    regrouped = regrouped.reshape(
        col_count, block_ratio, shard_rows, flagged.shape[1], flagged.shape[2]
    )
    second_side = jnp.transpose(regrouped, (1, 0, 2, 3, 4)).reshape(
        -1, flagged.shape[1], flagged.shape[2]
    )
    col_stack = jnp.stack([second_side, swap_parts(second_side, half_width)])
    row_stack = jnp.stack([first_side, -swap_parts(first_side, half_width)])
    cross_spec = jnp.einsum(
        "ifk,cjfk->cfij", first_side, col_stack, preferred_element_type=jnp.float32
    )
    residual = (
        pair_mask.astype(jnp.float32)[None, None]
        * misfit_weight.astype(jnp.float32)[None]
        * (cross_spec - observed.astype(jnp.float32))
    ).astype(jnp.bfloat16)
    residual_part = residual
    grad_first = summed_on_arrival(
        jnp.einsum(
            "cfij,cjfk->ifk", residual_part, col_stack, preferred_element_type=jnp.float32
        ).astype(jnp.bfloat16),
        "col",
        0,
    )
    residual_part = residual
    grad_second = summed_on_arrival(
        jnp.einsum(
            "cfij,cifk->jfk", residual_part, row_stack, preferred_element_type=jnp.float32
        ).astype(jnp.bfloat16),
        "row",
        0,
    )
    return (grad_first.astype(jnp.bfloat16), grad_second.astype(jnp.bfloat16)[None])


def solution(mesh):
    placed = (
        P(("row", "col"), None, None),
        P(("row", "col"), None),
        P("row", "col"),
        P(None, "row", "col"),
        P(None, None, "row", "col"),
    )
    return jax.shard_map(
        per_device,
        mesh=mesh,
        in_specs=placed,
        out_specs=(P(("row", "col"), None, None), P("col", "row", None, None)),
        check_vma=False,
    )
```

profile of v0, /device:TPU:6, one launch (start us, length us, event | category | flops | bytes accessed | tf_op | source)
XLA Modules:
  0.0 168.6 jit_solution(9327703946264331099)
XLA Ops:
  0.6 0.7 convert_element_type.31
  1.4 0.8 broadcast_multiply_fusion
  2.2 0.2 broadcast_in_dim.12
  2.4 41.5 %all_to_all.25 = bf16[32,8,16,128]{3,2,1,0:T(8,128)(2,1)} all-to-all(bf16[32,8,16,128]{3,2,1,0:T(8,128)(2,1)S(1)} %broadcast_in_dim.12), channel_id=1, replica_groups=mesh['row'=32,'col'=16] {'row'}, dimensions={0} | all-to-all | bytes 2097152 | tf_op jit(solution)/shard_map/all_to_all | solution.py:9
  43.9 10.7 %all-to-all-start.1 = ((bf16[256,16,128]{2,1,0:T(8,128)(2,1)}), bf16[256,16,128]{2,1,0:T(8,128)(2,1)S(1)}, u32[]{:S(2)}, u32[]{:S(2)}) async-start(bf16[256,16,128]{2,1,0:T(8,128)(2,1)} %bitcast), calls=%async_computation.1 | async-start | bytes 2097152 | tf_op jit(solution)/shard_map/all_to_all | solution.py:46
  54.5 19.2 %all-to-all-done.1 = bf16[256,16,128]{2,1,0:T(8,128)(2,1)S(1)} async-done(((bf16[256,16,128]{2,1,0:T(8,128)(2,1)}), bf16[256,16,128]{2,1,0:T(8,128)(2,1)S(1)}, u32[]{:S(2)}, u32[]{:S(2)}) %all-to-all-start.1) | async-done | bytes 1048608 | tf_op jit(solution)/shard_map/all_to_all | solution.py:46
  73.8 1.0 broadcast_in_dim.13
  74.8 5.9 %all-to-all-start.2 = ((bf16[16,8,16,128]{3,1,2,0:T(8,128)(2,1)}), bf16[16,8,16,128]{3,1,2,0:T(8,128)(2,1)}, u32[]{:S(2)}, u32[]{:S(2)}) async-start(bf16[16,8,16,128]{3,1,2,0:T(8,128)(2,1)} %broadcast_in_dim.13), calls=%async_computation.2 | async-start | bytes 1048576 | tf_op jit(solution)/shard_map/all_to_all | solution.py:9
  80.7 1.6 convert_multiply_fusion
  82.3 1.9 %copy.24 = f32[16,128,256]{1,2,0:T(8,128)S(1)} copy(f32[16,128,256]{2,1,0:T(8,128)} %convert_multiply_fusion) | data formatting | bytes 4194304 | tf_op jit(solution)/shard_map/mul | solution.py:61
  84.2 4.0 %copy.27 = bf16[2,16,128,256]{2,3,0,1:T(8,128)(2,1)} copy(bf16[2,16,128,256]{3,2,1,0:T(8,128)(2,1)} %param.9) | data formatting | bytes 4194304 | tf_op args[4]
  88.2 1.5 copy.22
  89.7 0.4 slice_negate_fusion
  90.1 1.6 maximum_bitcast_fusion
  91.7 1.6 all-to-all-done.2
  93.3 3.0 %fusion.1 = bf16[2,16,128,256]{2,3,0,1:T(8,128)(2,1)S(1)} fusion(bf16[2,16,128,256]{2,3,0,1:T(8,128)(2,1)} %copy.27, f32[16,128,256]{1,2,0:T(8,128)S(1)} %copy.24, bf16[1,256,16,128]{3,1,0,2:T(8,128)(2,1)} %maximum_bitcast_fusion, bf16[1,256,16,128]{3,1,0,2:T(8,128)(2,1)S(1)} %bitcast.50, bf16[16,8,16,128]{3,1,2,0:T(8,128)(2,1)} %all-to-all-done.2), kind=kOutput, calls=%fused_computation.2 | convolution fusion | flops 273678336 | bytes 8912896 | tf_op jit(solution)/shard_map/ifk,cjfk->cfij/dot_general | solution.py:57
  96.3 0.8 fusion.10
  97.2 0.5 copy-done.2
  97.6 0.9 copy.29
  98.6 8.0 %all-to-all-start.3 = ((bf16[16,8,16,128]{3,1,2,0:T(8,128)(2,1)}), bf16[16,8,16,128]{3,1,2,0:T(8,128)(2,1)S(1)}, u32[]{:S(2)}, u32[]{:S(2)}) async-start(bf16[16,8,16,128]{3,1,2,0:T(8,128)(2,1)} %copy.29), calls=%async_computation.3 | async-start | bytes 1048576 | tf_op jit(solution)/shard_map/all_to_all | solution.py:30
  106.6 1.2 copy.55
  107.8 0.2 fusion.14
  108.0 0.3 maximum_negate_fusion
  108.4 1.0 copy-done.3
  109.4 0.8 fusion.6
  110.2 1.8 %copy.34 = bf16[256,16,128]{2,1,0:T(8,128)(2,1)} copy(bf16[256,16,128]{0,2,1:T(8,128)(2,1)S(1)} %fusion.6) | data formatting | bytes 2097152 | tf_op jit(solution)/shard_map/convert_element_type | solution.py:77
  112.0 7.1 %all-to-all-done.3 = bf16[16,8,16,128]{3,1,2,0:T(8,128)(2,1)S(1)} async-done(((bf16[16,8,16,128]{3,1,2,0:T(8,128)(2,1)}), bf16[16,8,16,128]{3,1,2,0:T(8,128)(2,1)S(1)}, u32[]{:S(2)}, u32[]{:S(2)}) %all-to-all-start.3) | async-done | bytes 524320 | tf_op jit(solution)/shard_map/all_to_all | solution.py:30
  119.1 20.4 %all-to-all-start.4 = ((bf16[32,8,16,128]{3,2,1,0:T(8,128)(2,1)}), bf16[32,8,16,128]{3,2,1,0:T(8,128)(2,1)S(1)}, u32[]{:S(2)}, u32[]{:S(2)}) async-start(bf16[32,8,16,128]{3,2,1,0:T(8,128)(2,1)} %bitcast.20), calls=%async_computation.4 | async-start | bytes 2097152 | tf_op jit(solution)/shard_map/all_to_all | solution.py:30
  139.5 0.1 reduce_sum.24
  139.6 0.6 copy.35
  140.2 27.6 %all-to-all-done.4 = bf16[32,8,16,128]{3,2,1,0:T(8,128)(2,1)S(1)} async-done(((bf16[32,8,16,128]{3,2,1,0:T(8,128)(2,1)}), bf16[32,8,16,128]{3,2,1,0:T(8,128)(2,1)S(1)}, u32[]{:S(2)}, u32[]{:S(2)}) %all-to-all-start.4) | async-done | bytes 1048608 | tf_op jit(solution)/shard_map/all_to_all | solution.py:30
  167.8 0.8 reduce_sum.25
  (13 shorter events, 0.1 us)
Async XLA Ops:
  43.9 36.8 %copy-start.5 = (s32[128,256]{1,0:T(8,128)S(1)}, s32[128,256]{1,0:T(8,128)}, u32[]{:S(2)}) copy-start(s32[128,256]{1,0:T(8,128)} %param.7) | copy-start | bytes 393220
  43.9 36.8 %copy-start.4 = (bf16[16,128,256]{2,1,0:T(8,128)(2,1)S(1)}, bf16[16,128,256]{2,1,0:T(8,128)(2,1)}, u32[]{:S(2)}) copy-start(bf16[16,128,256]{2,1,0:T(8,128)(2,1)} %param.8) | copy-start | bytes 3145732
  43.9 29.9 %all-to-all-start.1 = ((bf16[256,16,128]{2,1,0:T(8,128)(2,1)}), bf16[256,16,128]{2,1,0:T(8,128)(2,1)S(1)}, u32[]{:S(2)}, u32[]{:S(2)}) async-start(bf16[256,16,128]{2,1,0:T(8,128)(2,1)} %bitcast), calls=%async_computation.1 | async-start | bytes 2097152 | tf_op jit(solution)/shard_map/all_to_all | solution.py:46
  73.8 8.5 %copy-start.1 = (bf16[256,16,128]{2,1,0:T(8,128)(2,1)}, bf16[256,16,128]{2,1,0:T(8,128)(2,1)S(1)}, u32[]{:S(2)}) copy-start(bf16[256,16,128]{2,1,0:T(8,128)(2,1)S(1)} %all-to-all-done.1) | copy-start | bytes 3145732
  74.8 18.5 %all-to-all-start.2 = ((bf16[16,8,16,128]{3,1,2,0:T(8,128)(2,1)}), bf16[16,8,16,128]{3,1,2,0:T(8,128)(2,1)}, u32[]{:S(2)}, u32[]{:S(2)}) async-start(bf16[16,8,16,128]{3,1,2,0:T(8,128)(2,1)} %broadcast_in_dim.13), calls=%async_computation.2 | async-start | bytes 1048576 | tf_op jit(solution)/shard_map/all_to_all | solution.py:9
  93.3 3.0 %copy-start = (bf16[1,256,16,128]{3,1,0,2:T(8,128)(2,1)S(1)}, bf16[1,256,16,128]{3,1,0,2:T(8,128)(2,1)}, u32[]{:S(2)}) copy-start(bf16[1,256,16,128]{3,1,0,2:T(8,128)(2,1)} %maximum_bitcast_fusion) | copy-start | bytes 3145732
  96.3 1.3 copy-start.2
  98.6 20.5 %all-to-all-start.3 = ((bf16[16,8,16,128]{3,1,2,0:T(8,128)(2,1)}), bf16[16,8,16,128]{3,1,2,0:T(8,128)(2,1)S(1)}, u32[]{:S(2)}, u32[]{:S(2)}) async-start(bf16[16,8,16,128]{3,1,2,0:T(8,128)(2,1)} %copy.29), calls=%async_computation.3 | async-start | bytes 1048576 | tf_op jit(solution)/shard_map/all_to_all | solution.py:30
  107.8 1.6 copy-start.3
  119.1 48.7 %all-to-all-start.4 = ((bf16[32,8,16,128]{3,2,1,0:T(8,128)(2,1)}), bf16[32,8,16,128]{3,2,1,0:T(8,128)(2,1)S(1)}, u32[]{:S(2)}, u32[]{:S(2)}) async-start(bf16[32,8,16,128]{3,2,1,0:T(8,128)(2,1)} %bitcast.20), calls=%async_computation.4 | async-start | bytes 2097152 | tf_op jit(solution)/shard_map/all_to_all | solution.py:30
where the time goes:
time: 171 us; the launch traced here: 169 us
  waiting for transfers between devices  55.6 us (33%)
  starting transfers between devices  44.9 us (26%)
  blocking collectives  41.5 us (24%)
  local copies, waits for them, and re-layouts  14.6 us (9%)
  other arithmetic  6.53 us (4%)
  matrix products  4.64 us (3%)
    all_to_all x1, blocking collectives, from_everyone(): return lax.all_to_all(copies, axis, split_axis=0, concat_axis=0, tiled=True)  41.5 us
    all_to_all x2, waiting for transfers between devices, summed_on_arrival(): lax.all_to_all(blocks, axis, split_axis=0, concat_axis=0, tiled=True)  34.7 us
    all_to_all x2, starting transfers between devices, summed_on_arrival(): lax.all_to_all(blocks, axis, split_axis=0, concat_axis=0, tiled=True)  28.4 us
    all_to_all x1, waiting for transfers between devices, per_device(): lax.all_to_all(strided, 'col', split_axis=0, concat_axis=0, tiled=True)  19.2 us
    all_to_all x1, starting transfers between devices, per_device(): lax.all_to_all(strided, 'col', split_axis=0, concat_axis=0, tiled=True)  10.7 us
    unnamed x14, local copies, waits for them, and re-layouts  6.09 us
    all_to_all x1, starting transfers between devices, from_everyone(): return lax.all_to_all(copies, axis, split_axis=0, concat_axis=0, tiled=True)  5.88 us
  transfers between devices with their start and end apart: 4, of which 4 were waited for; matrix products, arithmetic and copies ran while one was open for 9% of the time, Pallas kernels for 0%

commit v1 on v0

v1 whole, which is shorter than its diff:
```python
import jax
import jax.numpy as jnp
from jax import lax
from jax.experimental import pallas as pl
from jax.experimental.pallas import tpu as pltpu
from jax.sharding import PartitionSpec as P

MESH = pl.DeviceIdType.MESH
BF = jnp.bfloat16
F32 = jnp.float32
F = 16
K = 128
CHIPS = 8
YS = 8
ZS = 4
HALF = F // 2
STREAMS = ((1, 0, 4), (-1, 1, 4), (1, 1, 3), (-1, 0, 3))
FIRST = (0, 4, 8, 11)
MESSAGES = 14


def shift_of(here, there):
    hi = lax.rem(here // 4 + there // 4, 2)
    dx = lax.rem(here - there + 8, 4)
    same = 4 - dx + 4 * (dx // 2)
    other = lax.rem(2 - dx + 8, 8)
    return hi * other + (1 - hi) * same


def chip_at(there, y):
    dy = lax.rem(y - there + 8, 8)
    hi = 1 - lax.rem(dy + 1, 8) // 4
    dx = lax.rem(hi * 2 + (1 - hi) * 4 - dy + 8, 4)
    return lax.rem(there // 4 + hi, 2) * 4 + lax.rem(there + dx, 4)


def kernel(
    spectra, flags, mask, weight, observed, grad_first, grad_second,
    spec_v, flag_v, mask_v, weight_v, obs_v, turn, mine, first, second,
    gf_own, gf_got, gf_sum, gf_in, gs_own, gs_got, gz_own, gz_in,
    load_sem, put_s, put_r, hi_s, hi_r, x_s, x_r, pair_s, pair_r, ring_s, ring_r,
    gp_s, gp_r, gx_s, gx_r, red_s, red_r, z_s, z_r,
):
    row = lax.axis_index("row")
    col = lax.axis_index("col")
    y, zl = row // ZS, lax.rem(row, ZS)
    chip, core = col // 2, lax.rem(col, 2)
    hi, x = chip // 4, lax.rem(chip, 4)

    def device(y, zl, chip, core):
        return (y * ZS + zl, chip * 2 + core)

    def step_y(n):
        return lax.rem(y + n + 2 * YS, YS)

    def remote(src, dst, send, recv, to):
        return pltpu.make_async_remote_copy(
            src_ref=src, dst_ref=dst, send_sem=send, recv_sem=recv, device_id=to, device_id_type=MESH
        )

    loads = [
        pltpu.make_async_copy(a, b, load_sem.at[n])
        for n, (a, b) in enumerate(
            ((spectra, spec_v), (flags, flag_v), (mask, mask_v), (weight, weight_v), (observed, obs_v))
        )
    ]
    for load in loads:
        load.start()

    barrier = pltpu.get_barrier_semaphore()
    partner = device(y, zl, chip, 1 - core)
    peers = [partner]
    peers += [device(y, zl, lax.rem(chip + n, CHIPS), core) for n in range(1, CHIPS)]
    peers += [device(step_y(n), zl, chip, core) for n in (1, -1)]
    peers += [device(y, lax.rem(zl + n, ZS), chip, core) for n in range(1, ZS)]
    giver = chip_at(chip, y)
    peers += [device(chip, 2 * core + b, giver, c) for b in range(2) for c in range(2)]
    for peer in peers:
        pl.semaphore_signal(barrier, inc=1, device_id=peer, device_id_type=MESH)

    loads[0].wait()
    loads[1].wait()
    turn[...] = spec_v[...].astype(F32).reshape(8 * F, K)
    flag = flag_v[...].astype(F32)
    flag = jnp.concatenate([flag, flag], axis=1)
    pieces = [(turn[pl.ds(f, 8, stride=F), :] * flag).astype(BF) for f in range(F)]
    for f in range(F):
        mine[f] = pieces[f]

    for c in range(2):

        @pl.when(core == c)
        def _():
            for f in range(F):
                first[chip, f, 8 * c : 8 * c + 8, :] = pieces[f]

    pl.semaphore_wait(barrier, len(peers))

    def eight(c):
        return pl.ds(pl.multiple_of(c * 8, 8), 8)

    to_y = lax.rem(y + shift_of(chip, y), YS)
    puts = []
    for n in range(ZS):
        puts.append(
            remote(
                mine,
                second.at[chip, :, lax.rem(zl, 2), eight(core), :],
                put_s.at[n],
                put_r.at[lax.rem(zl, 2) * 2 + core],
                device(to_y, lax.rem(zl + n, ZS), y, zl // 2),
            )
        )
        puts[-1].start()

    far = lax.rem(hi + 1, 2) * 4 + x
    cross_hi = remote(mine, first.at[chip, :, eight(core), :], hi_s, hi_r, device(y, zl, far, core))
    cross_hi.start()
    along_x = []
    for n in range(1, 4):
        to = device(y, zl, hi * 4 + lax.rem(x + n, 4), core)
        along_x.append(remote(mine, first.at[chip, :, eight(core), :], x_s.at[n - 1], x_r.at[n - 1], to))
        along_x[-1].start()

    for b in range(2):
        for c in range(2):
            n = b * 2 + c
            remote(mine, second.at[giver, :, b, 8 * c : 8 * c + 8, :], put_s.at[n], put_r.at[n], partner).wait_recv()

    def ring_copy(s, t):
        way, half, steps = STREAMS[s]
        block = second.at[chip_at(chip, step_y(-way * (t - 1))), half * HALF : half * HALF + HALF]
        n = FIRST[s] + t - 1
        return remote(block, block, ring_s.at[n], ring_r.at[n], device(step_y(way), zl, chip, core))

    def ring_arrival(s, t):
        way, half, steps = STREAMS[s]
        block = second.at[chip_at(chip, step_y(-way * t)), half * HALF : half * HALF + HALF]
        n = FIRST[s] + t - 1
        return remote(block, block, ring_s.at[n], ring_r.at[n], device(step_y(way), zl, chip, core))

    ring = []
    for s in range(4):
        ring.append(ring_copy(s, 1))
        ring[-1].start()

    remote(mine, first.at[far, :, eight(core), :], hi_s, hi_r, partner).wait_recv()
    for n in range(1, 4):
        to = device(y, zl, hi * 4 + lax.rem(x + n, 4), core)
        block = first.at[far, :, eight(core), :]
        along_x.append(remote(block, block, x_s.at[n + 2], x_r.at[n + 2], to))
        along_x[-1].start()

    def ring_step(t):
        for s in range(4):
            if t <= STREAMS[s][2]:
                ring_arrival(s, t - 1).wait_recv()
                ring.append(ring_copy(s, t))
                ring[-1].start()

    ring_step(2)

    pair = []
    for g in range(2):
        for n in range(1, 4):
            from_chip = (hi if g == 0 else lax.rem(hi + 1, 2)) * 4 + lax.rem(x - n + 4, 4)
            m = g * 3 + n - 1
            remote(mine, first.at[from_chip, :, eight(core), :], x_s.at[m], x_r.at[m], partner).wait_recv()
    block = first.at[:, :, eight(core), :]
    pair.append(remote(block, block, pair_s, pair_r, partner))
    pair[-1].start()

    ring_step(3)
    ring_step(4)
    other = first.at[:, :, eight(1 - core), :]
    remote(other, other, pair_s, pair_r, partner).wait_recv()
    for load in loads[2:]:
        load.wait()
    for s in range(4):
        ring_arrival(s, STREAMS[s][2]).wait_recv()

    lane = lax.broadcasted_iota(jnp.int32, (1, K), 1)
    sign = jnp.where(lane < K // 2, 1.0, -1.0).astype(F32)

    def one_frequency(f, carry):
        v = first[:, f].reshape(128, K)
        turned = (pltpu.roll(v.astype(F32), K // 2, 1) * sign).astype(BF)
        rows = jnp.concatenate([v, turned], axis=0)
        cols = jnp.concatenate([second[:, f, b].reshape(128, K) for b in range(2)], axis=0)
        cross = lax.dot_general(rows, cols, (((1,), (1,)), ((), ())), preferred_element_type=F32)
        scale = mask_v[...].astype(F32) * weight_v[f].astype(F32)
        residual = jnp.concatenate(
            [(scale * (cross[128 * c : 128 * c + 128] - obs_v[c, f].astype(F32))).astype(BF) for c in range(2)], axis=0
        )
        prod = jnp.dot(residual, cols, preferred_element_type=F32)
        gf = prod[:128] - pltpu.roll(prod[128:], K // 2, 1) * sign
        gf = gf.reshape(CHIPS, 2, 8, K)
        for c in range(2):
            gf_own[c, :, f] = gf[:, c].astype(BF)
        gs = lax.dot_general(residual, rows, (((0,), (0,)), ((), ())), preferred_element_type=F32)
        gs_own[:, f] = gs.reshape(YS, 32, K).astype(BF)
        return carry

    lax.fori_loop(0, F, one_frequency, 0)

    def half_of(ref, half):
        return ref.at[half * HALF : half * HALF + HALF]

    def red_copy(s, t):
        way, half, steps = STREAMS[s]
        n = FIRST[s] + t - 1
        src = half_of(gs_own.at[step_y(way * (steps - t + 1))], half)
        return remote(src, gs_got.at[n], red_s.at[n], red_r.at[n], device(step_y(way), zl, chip, core))

    red = []
    for s in range(4):
        red.append(red_copy(s, 1))
        red[-1].start()

    gpair = remote(gf_own.at[1 - core], gf_got, gp_s, gp_r, partner)
    gpair.start()

    def red_step(t):
        for s in range(4):
            way, half, steps = STREAMS[s]
            if t <= steps:
                n = FIRST[s] + t - 2
                red_copy(s, t - 1).wait_recv()
                acc = gs_own.at[step_y(way * (steps - t + 1))]
                span = slice(half * HALF, half * HALF + HALF)
                acc[span] = (acc[span].astype(F32) + gs_got[n].astype(F32)).astype(BF)
                red.append(red_copy(s, t))
                red[-1].start()

    gpair.wait_recv()
    gf_sum[...] = (gf_own[core].astype(F32) + gf_got[...].astype(F32)).astype(BF)
    spread = []
    for n in range(1, CHIPS):
        to = lax.rem(chip + n, CHIPS)
        spread.append(
            remote(gf_sum.at[to], gf_in.at[n - 1], gx_s.at[n - 1], gx_r.at[n - 1], device(y, zl, to, core))
        )
        spread[-1].start()

    red_step(2)
    red_step(3)
    red_step(4)

    total = gs_own[y].astype(F32)
    parts = []
    for half in range(2):
        part = gs_own[y, half * HALF : half * HALF + HALF].astype(F32)
        for s in range(4):
            if STREAMS[s][1] == half:
                red_copy(s, STREAMS[s][2]).wait_recv()
                part = part + gs_got[FIRST[s] + STREAMS[s][2] - 1].astype(F32)
        parts.append(part)
    total = jnp.concatenate(parts, axis=0).reshape(F, ZS, 8, K)
    for n in range(ZS):
        gz_own[n] = total[:, n].astype(BF)
    down = []
    for n in range(1, ZS):
        to = lax.rem(zl + n, ZS)
        down.append(remote(gz_own.at[to], gz_in.at[n - 1], z_s.at[n - 1], z_r.at[n - 1], device(y, to, chip, core)))
        down[-1].start()

    def put_out(value, out):
        turn[...] = value.reshape(8 * F, K)
        for s in range(8):
            out[s] = turn[pl.ds(s, F, stride=8), :].astype(BF)

    value = gf_sum[chip].astype(F32)
    for n in range(CHIPS - 1):
        spread[n].wait_recv()
        value = value + gf_in[n].astype(F32)
    put_out(value, grad_first)

    value = gz_own[zl].astype(F32)
    for n in range(ZS - 1):
        down[n].wait_recv()
        value = value + gz_in[n].astype(F32)
    put_out(value, grad_second.at[0])

    for copy in puts + [cross_hi] + along_x + ring + pair + red + [gpair] + spread + down:
        copy.wait_send()


def per_device(spectra, window_flags, pair_mask, misfit_weight, observed):
    dma = pltpu.SemaphoreType.DMA
    vmem = pltpu.VMEM
    return pl.pallas_call(
        kernel,
        out_shape=(
            jax.ShapeDtypeStruct((8, F, K), BF),
            jax.ShapeDtypeStruct((1, 8, F, K), BF),
        ),
        in_specs=[pl.BlockSpec(memory_space=pl.ANY)] * 5,
        out_specs=[pl.BlockSpec(memory_space=pltpu.VMEM)] * 2,
        scratch_shapes=[
            vmem((8, F, K), BF),
            vmem((8, K // 2), jnp.int32),
            vmem((128, 256), jnp.int32),
            vmem((F, 128, 256), BF),
            vmem((2, F, 128, 256), BF),
            vmem((8 * F, K), F32),
            vmem((F, 8, K), BF),
            vmem((CHIPS, F, 16, K), BF),
            vmem((CHIPS, F, 2, 16, K), BF),
            vmem((2, CHIPS, F, 8, K), BF),
            vmem((CHIPS, F, 8, K), BF),
            vmem((CHIPS, F, 8, K), BF),
            vmem((CHIPS - 1, F, 8, K), BF),
            vmem((YS, F, 32, K), BF),
            vmem((MESSAGES, HALF, 32, K), BF),
            vmem((ZS, F, 8, K), BF),
            vmem((ZS - 1, F, 8, K), BF),
            dma((5,)),
            dma((4,)), dma((4,)),
            dma, dma,
            dma((6,)), dma((6,)),
            dma, dma,
            dma((MESSAGES,)), dma((MESSAGES,)),
            dma, dma,
            dma((7,)), dma((7,)),
            dma((MESSAGES,)), dma((MESSAGES,)),
            dma((3,)), dma((3,)),
        ],
        compiler_params=pltpu.CompilerParams(collective_id=0, has_side_effects=True),
    )(spectra, window_flags, pair_mask, misfit_weight, observed)


def solution(mesh):
    placed = (
        P(("row", "col"), None, None),
        P(("row", "col"), None),
        P("row", "col"),
        P(None, "row", "col"),
        P(None, None, "row", "col"),
    )
    return jax.shard_map(
        per_device,
        mesh=mesh,
        in_specs=placed,
        out_specs=(P(("row", "col"), None, None), P("col", "row", None, None)),
        check_vma=False,
    )
```

time: 171 us -> 73.5 us (0.43); the launches traced: 169 us -> 73.2 us
  Pallas kernels: 0 us -> 69.9 us
  waiting for transfers between devices: 55.6 us -> 0 us
  starting transfers between devices: 44.9 us -> 0 us
  blocking collectives: 41.5 us -> 0 us
  local copies, waits for them, and re-layouts: 14.6 us -> 2.75 us
  other arithmetic: 6.53 us -> 0 us
  matrix products: 4.64 us -> 0 us
    pallas_call x0 -> x1, Pallas kernels: none -> 69.9 us  [per_device(): pl.pallas_call(kernel, out_shape=(jax.ShapeDtypeStruct((8, F, K), BF), ja...]
    all_to_all x4 -> x0, waiting for transfers between devices: 55.6 us -> none  [the longest x2 34.7 us: summed_on_arrival(): lax.all_to_all(blocks, axis, split_axis=0, concat_axis=0, tiled=True)]
    all_to_all x4 -> x0, starting transfers between devices: 44.9 us -> none  [the longest x2 28.4 us: summed_on_arrival(): lax.all_to_all(blocks, axis, split_axis=0, concat_axis=0, tiled=True)]
    all_to_all x1 -> x0, blocking collectives: 41.5 us -> none  [from_everyone(): return lax.all_to_all(copies, axis, split_axis=0, concat_axis=0, tiled=True)]
    dot_general x3 -> x0, matrix products: 4.64 us -> none  [the longest x1 2.97 us: per_device(): jnp.einsum('ifk,cjfk->cfij', first_side, col_stack, preferred_element_typ...]
    unnamed x14 -> x2, local copies, waits for them, and re-layouts: 6.09 us -> 2.75 us
    mul x2 -> x0, other arithmetic: 2.34 us -> none  [the longest x1 1.57 us: per_device(): pair_mask.astype(jnp.float32)[None, None]]
    mul x2 -> x0, local copies, waits for them, and re-layouts: 1.92 us -> none  [the longest x1 1.91 us: per_device(): pair_mask.astype(jnp.float32)[None, None]]
  transfers between devices with their start and end apart: 4 -> 0, of which waited for: 4 -> 0; matrix products, arithmetic and copies ran while one was open for 9% -> 0% of each run, Pallas kernels for 0% -> 0%
where the time goes in v1:
time: 73.5 us; the launch traced here: 73.2 us
  Pallas kernels  69.9 us (95%)
  local copies, waits for them, and re-layouts  2.75 us (4%)
    pallas_call x1, Pallas kernels, per_device(): pl.pallas_call(kernel, out_shape=(jax.ShapeDtypeStruct((8, F, K), BF), ja...  69.9 us
    unnamed x2, local copies, waits for them, and re-layouts  2.75 us

profile of v1, /device:TPU:6, one launch (start us, length us, event | category | flops | bytes accessed | tf_op | source)
XLA Modules:
  0.0 73.2 jit_solution(4976533744825810105)
XLA Ops:
  0.6 69.9 %shard_map.68 = (bf16[8,16,128]{2,1,0:T(8,128)(2,1)}, bf16[1,8,16,128]{3,2,1,0:T(8,128)(2,1)}) custom-call(bf16[8,16,128]{2,1,0:T(8,128)(2,1)} %spectra.1, s32[8,64]{1,0:T(8,128)} %flags.1, s32[128,256]{1,0:T(8,128)} %mask.1, bf16[16,128,256]{2,1,0:T(8,128)(2,1)} %weight.1, bf16[2,16,128,256]{3,2,1,0:T(8,128)(2,1)} %observed.1), custom_call_target="tpu_custom_call" | custom-call | tf_op jit(solution)/shard_map/pallas_call | solution.py:291
  70.5 1.4 %copy.9 = bf16[8,16,128]{2,1,0:T(8,128)(2,1)} copy(bf16[8,16,128]{2,1,0:T(8,128)(2,1)} %get-tuple-element.4) | data formatting | bytes 65536
  71.9 1.4 %copy.10 = bf16[1,8,16,128]{3,2,1,0:T(8,128)(2,1)} copy(bf16[1,8,16,128]{3,2,1,0:T(8,128)(2,1)} %get-tuple-element.5) | data formatting | bytes 65536

commit v2 on v1

v2 whole, which is shorter than its diff:
```python
import jax
import jax.numpy as jnp
from jax import lax
from jax.experimental import pallas as pl
from jax.experimental.pallas import tpu as pltpu
from jax.sharding import PartitionSpec as P

MESH = pl.DeviceIdType.MESH
BF = jnp.bfloat16
F32 = jnp.float32
F = 16
K = 128
CHIPS = 8
YS = 8
ZS = 4
GROUPS = 4
G = F // GROUPS
HALF = F // 2
UNROLL = 2
WAYS = (1, -1)


def steps_of(group, way):
    return 4 if (group + way) % 2 == 0 else 3


MESSAGE = {}
for _g in range(GROUPS):
    for _w in range(2):
        for _t in range(1, steps_of(_g, _w) + 1):
            MESSAGE[_g, _w, _t] = len(MESSAGE)
MESSAGES = len(MESSAGE)


def shift_of(here, there):
    hi = lax.rem(here // 4 + there // 4, 2)
    dx = lax.rem(here - there + 8, 4)
    same = 4 - dx + 4 * (dx // 2)
    other = lax.rem(2 - dx + 8, 8)
    return hi * other + (1 - hi) * same


def chip_at(there, y):
    dy = lax.rem(y - there + 8, 8)
    hi = 1 - lax.rem(dy + 1, 8) // 4
    dx = lax.rem(hi * 2 + (1 - hi) * 4 - dy + 8, 4)
    return lax.rem(there // 4 + hi, 2) * 4 + lax.rem(there + dx, 4)


def kernel(
    spectra, flags, mask, weight, observed, out,
    spec_v, flag_v, mask_v, weight_v, obs_v, turn, mine, first, second,
    gf_own, gf_got, gf_sum, gf_in, gh_own, gh_in, gs_own, gs_got, gz_own, gz_in,
    load_sem, put_s, put_r, zs_s, zs_r, hi_s, hi_r, x_s, x_r, pair_s, pair_r, ring_s, ring_r,
    gp_s, gp_r, gx_s, gx_r, gh_s, gh_r, red_s, red_r, z_s, z_r,
):
    row = lax.axis_index("row")
    col = lax.axis_index("col")
    y, zl = row // ZS, lax.rem(row, ZS)
    chip, core = col // 2, lax.rem(col, 2)
    hi, x = chip // 4, lax.rem(chip, 4)

    def device(y, zl, chip, core):
        return (y * ZS + zl, chip * 2 + core)

    def step_y(n):
        return lax.rem(y + n + 2 * YS, YS)

    sent = []

    def remote(src, dst, send, recv, to):
        return pltpu.make_async_remote_copy(
            src_ref=src, dst_ref=dst, send_sem=send, recv_sem=recv, device_id=to, device_id_type=MESH
        )

    def send(*args):
        sent.append(remote(*args))
        sent[-1].start()

    def group(g):
        return slice(g * G, g * G + G)

    def half(n):
        return slice(n * HALF, n * HALF + HALF)

    def eight(c):
        return pl.ds(pl.multiple_of(c * 8, 8), 8)

    loads = [
        pltpu.make_async_copy(a, b, load_sem.at[n])
        for n, (a, b) in enumerate(
            ((spectra, spec_v), (flags, flag_v), (mask, mask_v), (weight, weight_v), (observed, obs_v))
        )
    ]
    loads[0].start()
    loads[1].start()

    barrier = pltpu.get_barrier_semaphore()
    partner = device(y, zl, chip, 1 - core)
    far = lax.rem(hi + 1, 2) * 4 + x
    giver = chip_at(chip, y)
    holder = zl // 2 == core
    row_chips = [device(y, zl, hi * 4 + lax.rem(x + n, 4), core) for n in range(1, 4)]
    z_line = [device(y, lax.rem(zl + n, ZS), chip, core) for n in range(1, ZS)]
    peers = [partner, device(y, zl, far, core)] + row_chips + z_line
    peers += [device(step_y(way), zl, chip, core) for way in WAYS]
    for peer in peers:
        pl.semaphore_signal(barrier, inc=1, device_id=peer, device_id_type=MESH)

    @pl.when(holder)
    def _():
        for c in range(2):
            pl.semaphore_signal(barrier, inc=1, device_id=device(chip, zl, giver, c), device_id_type=MESH)

    for load in loads[2:]:
        load.start()

    loads[0].wait()
    loads[1].wait()
    turn[...] = spec_v[...].astype(F32).reshape(8 * F, K)
    flag = flag_v[...].astype(F32)
    flag = jnp.concatenate([flag, flag], axis=1)
    pieces = [(turn[pl.ds(f, 8, stride=F), :] * flag).astype(BF) for f in range(F)]
    for f in range(F):
        mine[f] = pieces[f]

    for c in range(2):

        @pl.when(core == c)
        def _():
            for f in range(F):
                first[chip, f, 8 * c : 8 * c + 8, :] = pieces[f]

    pl.semaphore_wait(barrier, len(peers) + 1)

    to = device(lax.rem(y + shift_of(chip, y), YS), zl, y, zl // 2)
    send(mine, second.at[chip, :, lax.rem(zl, 2), eight(core), :], put_s, put_r.at[core], to)

    send(mine, first.at[chip, :, eight(core), :], hi_s, hi_r, device(y, zl, far, core))
    for n in range(3):
        send(mine, first.at[chip, :, eight(core), :], x_s.at[n], x_r.at[n], row_chips[n])

    def spread_copies(g):
        block = second.at[giver, group(g), lax.rem(zl, 2)]
        return [
            remote(block, block, zs_s.at[g * 3 + n], zs_r.at[g * 2 + lax.rem(zl, 2)], z_line[n]) for n in range(3)
        ]

    @pl.when(holder)
    def _():
        for c in range(2):
            remote(
                mine, second.at[giver, :, lax.rem(zl, 2), 8 * c : 8 * c + 8, :], put_s, put_r.at[c], partner
            ).wait_recv()
        for g in range(GROUPS):
            for copy in spread_copies(g):
                copy.start()

    def spread_arrival(g, b):
        block = second.at[giver, group(g), b]
        remote(block, block, zs_s.at[0], zs_r.at[g * 2 + b], partner).wait_recv()

    def ring_copy(g, w, t, arrival=0):
        way = WAYS[w]
        block = second.at[chip_at(chip, step_y(-way * (t - 1 + arrival))), group(g)]
        n = MESSAGE[g, w, t]
        return (block, block, ring_s.at[n], ring_r.at[n], device(step_y(way), zl, chip, core))

    def ring_step(t):
        for g in range(GROUPS):
            for w in range(2):
                if t <= steps_of(g, w):
                    remote(*ring_copy(g, w, t - 1, 1)).wait_recv()
                    send(*ring_copy(g, w, t))

    for g in range(GROUPS):

        @pl.when(holder)
        def _():
            spread_arrival(g, 1 - lax.rem(zl, 2))

        @pl.when(jnp.logical_not(holder))
        def _():
            spread_arrival(g, 0)
            spread_arrival(g, 1)

        for w in range(2):
            send(*ring_copy(g, w, 1))

    block = first.at[far, :, eight(core), :]
    remote(mine, block, hi_s, hi_r, partner).wait_recv()
    for n in range(3):
        send(block, block, x_s.at[n + 3], x_r.at[n + 3], row_chips[n])

    def to_partner(n):
        z_hi = hi if n == 0 else lax.rem(hi + 1, 2)
        for m in range(3):
            from_chip = z_hi * 4 + lax.rem(x - m - 1 + 4, 4)
            remote(
                mine, first.at[from_chip, :, eight(core), :], x_s.at[0], x_r.at[n * 3 + m], partner
            ).wait_recv()
        block = first.at[pl.ds(z_hi * 4, 4), :, eight(core), :]
        send(block, block, pair_s.at[n], pair_r.at[n], partner)

    ring_step(2)
    to_partner(0)
    ring_step(3)
    to_partner(1)
    ring_step(4)
    for n in range(2):
        z_hi = hi if n == 0 else lax.rem(hi + 1, 2)
        block = first.at[pl.ds(z_hi * 4, 4), :, eight(1 - core), :]
        remote(block, block, pair_s.at[n], pair_r.at[n], partner).wait_recv()
    for load in loads[2:]:
        load.wait()

    lane = lax.broadcasted_iota(jnp.int32, (1, K), 1)
    sign = jnp.where(lane < K // 2, 1.0, -1.0).astype(F32)

    def one_frequency(f):
        v = first[:, f].reshape(128, K)
        turned = (pltpu.roll(v.astype(F32), K // 2, 1) * sign).astype(BF)
        rows = jnp.concatenate([v, turned], axis=0)
        cols = jnp.concatenate([second[:, f, b].reshape(128, K) for b in range(2)], axis=0)
        cross = lax.dot_general(rows, cols, (((1,), (1,)), ((), ())), preferred_element_type=F32)
        scale = mask_v[...].astype(F32) * weight_v[f].astype(F32)
        residual = jnp.concatenate(
            [(scale * (cross[128 * c : 128 * c + 128] - obs_v[c, f].astype(F32))).astype(BF) for c in range(2)], axis=0
        )
        prod = jnp.dot(residual, cols, preferred_element_type=F32)
        gf = prod[:128] - pltpu.roll(prod[128:], K // 2, 1) * sign
        gf = gf.reshape(CHIPS, 2, 8, K)
        for c in range(2):
            gf_own[c, :, f] = gf[:, c].astype(BF)
        gs = lax.dot_general(residual, rows, (((0,), (0,)), ((), ())), preferred_element_type=F32)
        gs_own[:, f] = gs.reshape(YS, 32, K).astype(BF)

    def compute(g):
        for w in range(2):
            remote(*ring_copy(g, w, steps_of(g, w), 1)).wait_recv()

        def pair_of(n, carry):
            for m in range(UNROLL):
                one_frequency(g * G + n * UNROLL + m)
            return carry

        lax.fori_loop(0, G // UNROLL, pair_of, 0)

    def red_copy(g, w, t):
        way = WAYS[w]
        n = MESSAGE[g, w, t]
        src = gs_own.at[step_y(way * (steps_of(g, w) - t + 1)), group(g)]
        return (src, gs_got.at[n], red_s.at[n], red_r.at[n], device(step_y(way), zl, chip, core))

    def reduce(g, t):
        for w in range(2):
            steps = steps_of(g, w)
            if t > steps:
                continue
            if t > 1:
                remote(*red_copy(g, w, t - 1)).wait_recv()
                acc = gs_own.at[step_y(WAYS[w] * (steps - t + 1)), group(g)]
                acc[...] = (acc[...].astype(F32) + gs_got[MESSAGE[g, w, t - 1]].astype(F32)).astype(BF)
            send(*red_copy(g, w, t))

    def reduced(g):
        total = gs_own[y, group(g)].astype(F32)
        for w in range(2):
            steps = steps_of(g, w)
            remote(*red_copy(g, w, steps)).wait_recv()
            total = total + gs_got[MESSAGE[g, w, steps]].astype(F32)
        total = total.reshape(G, ZS, 8, K)
        for n in range(ZS):
            gz_own[n, group(g)] = total[:, n].astype(BF)
        for n in range(3):
            send(*z_copy(g, n))

    def z_copy(g, n):
        to = lax.rem(zl + n + 1, ZS)
        m = g * 3 + n
        return (gz_own.at[to, group(g)], gz_in.at[n, group(g)], z_s.at[m], z_r.at[m], z_line[n])

    def gf_pair(n):
        return (gf_own.at[1 - core, :, half(n)], gf_got.at[:, half(n)], gp_s.at[n], gp_r.at[n], partner)

    def gf_x(n, m):
        to = lax.rem(x + m + 1, 4)
        return (gf_sum.at[:, to, half(n)], gf_in.at[m, :, half(n)], gx_s.at[n * 3 + m], gx_r.at[n * 3 + m], row_chips[m])

    def gf_hi(n):
        return (gh_own.at[1 - hi, half(n)], gh_in.at[half(n)], gh_s.at[n], gh_r.at[n], device(y, zl, far, core))

    def gf_along_x(n):
        remote(*gf_pair(n)).wait_recv()
        value = gf_own[core, :, half(n)].astype(F32) + gf_got[:, half(n)].astype(F32)
        gf_sum[:, :, half(n)] = value.astype(BF).reshape(2, 4, HALF, 8, K)
        for m in range(3):
            send(*gf_x(n, m))

    def gf_across(n):
        value = gf_sum[:, x, half(n)].astype(F32)
        for m in range(3):
            remote(*gf_x(n, m)).wait_recv()
            value = value + gf_in[m, :, half(n)].astype(F32)
        gh_own[:, half(n)] = value.astype(BF)
        send(*gf_hi(n))

    compute(0)
    reduce(0, 1)
    compute(1)
    reduce(1, 1)
    send(*gf_pair(0))
    compute(2)
    reduce(2, 1)
    reduce(0, 2)
    gf_along_x(0)
    compute(3)
    reduce(3, 1)
    send(*gf_pair(1))
    reduce(1, 2)
    reduce(2, 2)
    reduce(0, 3)
    gf_along_x(1)
    reduce(3, 2)
    reduce(1, 3)
    gf_across(0)
    reduce(2, 3)
    reduce(0, 4)
    reduce(3, 3)
    reduce(1, 4)
    gf_across(1)
    reduce(2, 4)
    reduce(3, 4)
    for g in range(GROUPS):
        reduced(g)

    def put_out(value, out):
        turn[...] = value.reshape(8 * F, K)
        for s in range(8):
            out[s] = turn[pl.ds(s, F, stride=8), :].astype(BF)

    for n in range(2):
        remote(*gf_hi(n)).wait_recv()
    put_out(gh_own[hi].astype(F32) + gh_in[...].astype(F32), out.at[0])

    value = gz_own[zl].astype(F32)
    for n in range(3):
        for g in range(GROUPS):
            remote(*z_copy(g, n)).wait_recv()
        value = value + gz_in[n].astype(F32)
    put_out(value, out.at[1])

    for copy in sent:
        copy.wait_send()

    @pl.when(holder)
    def _():
        for g in range(GROUPS):
            for copy in spread_copies(g):
                copy.wait_send()


def finish(both, grad_first, grad_second):
    grad_first[...] = both[0]
    grad_second[0] = both[1]


def per_device(spectra, window_flags, pair_mask, misfit_weight, observed):
    dma = pltpu.SemaphoreType.DMA
    vmem = pltpu.VMEM
    both = pl.pallas_call(
        kernel,
        out_shape=jax.ShapeDtypeStruct((2, 8, F, K), BF),
        in_specs=[pl.BlockSpec(memory_space=pl.ANY)] * 5,
        out_specs=pl.BlockSpec(memory_space=pltpu.VMEM),
        scratch_shapes=[
            vmem((8, F, K), BF),
            vmem((8, K // 2), jnp.int32),
            vmem((128, 256), jnp.int32),
            vmem((F, 128, 256), BF),
            vmem((2, F, 128, 256), BF),
            vmem((8 * F, K), F32),
            vmem((F, 8, K), BF),
            vmem((CHIPS, F, 16, K), BF),
            vmem((CHIPS, F, 2, 16, K), BF),
            vmem((2, CHIPS, F, 8, K), BF),
            vmem((CHIPS, F, 8, K), BF),
            vmem((2, 4, F, 8, K), BF),
            vmem((3, 2, F, 8, K), BF),
            vmem((2, F, 8, K), BF),
            vmem((F, 8, K), BF),
            vmem((YS, F, 32, K), BF),
            vmem((MESSAGES, G, 32, K), BF),
            vmem((ZS, F, 8, K), BF),
            vmem((ZS - 1, F, 8, K), BF),
            dma((5,)),
            dma, dma((2,)),
            dma((3 * GROUPS,)), dma((2 * GROUPS,)),
            dma, dma,
            dma((6,)), dma((6,)),
            dma((2,)), dma((2,)),
            dma((MESSAGES,)), dma((MESSAGES,)),
            dma((2,)), dma((2,)),
            dma((6,)), dma((6,)),
            dma((2,)), dma((2,)),
            dma((MESSAGES,)), dma((MESSAGES,)),
            dma((3 * GROUPS,)), dma((3 * GROUPS,)),
        ],
        compiler_params=pltpu.CompilerParams(collective_id=0, has_side_effects=True),
    )(spectra, window_flags, pair_mask, misfit_weight, observed)
    return pl.pallas_call(
        finish,
        out_shape=(
            jax.ShapeDtypeStruct((8, F, K), BF),
            jax.ShapeDtypeStruct((1, 8, F, K), BF),
        ),
        in_specs=[pl.BlockSpec(memory_space=pltpu.VMEM)],
        out_specs=[pl.BlockSpec(memory_space=pltpu.VMEM)] * 2,
    )(both)


def solution(mesh):
    placed = (
        P(("row", "col"), None, None),
        P(("row", "col"), None),
        P("row", "col"),
        P(None, "row", "col"),
        P(None, None, "row", "col"),
    )
    return jax.shard_map(
        per_device,
        mesh=mesh,
        in_specs=placed,
        out_specs=(P(("row", "col"), None, None), P("col", "row", None, None)),
        check_vma=False,
    )
```

time: 73.5 us -> 62.7 us (0.85); the launches traced: 73.2 us -> 61.6 us
  Pallas kernels: 69.9 us -> 61 us
  local copies, waits for them, and re-layouts: 2.75 us -> 0 us
    pallas_call x1 -> x2, Pallas kernels: 69.9 us -> 61 us  [the longest x1 59.5 us: per_device(): pl.pallas_call(kernel, out_shape=jax.ShapeDtypeStruct((2, 8, F, K), BF),...]
    unnamed x2 -> x0, local copies, waits for them, and re-layouts: 2.75 us -> none
where the time goes in v2:
time: 62.7 us; the launch traced here: 61.6 us
  Pallas kernels  61 us (97%)
  between operations  0.64 us (1%)
    pallas_call x1, Pallas kernels, per_device(): pl.pallas_call(kernel, out_shape=jax.ShapeDtypeStruct((2, 8, F, K), BF),...  59.5 us
    pallas_call x1, Pallas kernels, per_device(): pl.pallas_call(finish, out_shape=(jax.ShapeDtypeStruct((8, F, K), BF), ja...  1.47 us

profile of v2, /device:TPU:6, one launch (start us, length us, event | category | flops | bytes accessed | tf_op | source)
XLA Modules:
  0.0 61.6 jit_solution(3415730707385388360)
XLA Ops:
  0.6 59.5 %shard_map.68.both = bf16[2,8,16,128]{3,2,1,0:T(8,128)(2,1)} custom-call(bf16[8,16,128]{2,1,0:T(8,128)(2,1)} %spectra.1, s32[8,64]{1,0:T(8,128)} %flags.1, s32[128,256]{1,0:T(8,128)} %mask.1, bf16[16,128,256]{2,1,0:T(8,128)(2,1)} %weight.1, bf16[2,16,128,256]{3,2,1,0:T(8,128)(2,1)} %observed.1), custom_call_target="tpu_custom_call" | custom-call | tf_op jit(solution)/shard_map/pallas_call | solution.py:371
  60.2 1.5 %shard_map.69 = (bf16[8,16,128]{2,1,0:T(8,128)(2,1)}, bf16[1,8,16,128]{3,2,1,0:T(8,128)(2,1)}) custom-call(bf16[2,8,16,128]{3,2,1,0:T(8,128)(2,1)} %shard_map.68.both), custom_call_target="tpu_custom_call" | custom-call | tf_op jit(solution)/shard_map/pallas_call | solution.py:411

commit v3 on v2

--- a/solution.py
+++ b/solution.py
@@ -1,3 +1,5 @@
+import functools
+
 import jax
 import jax.numpy as jnp
 from jax import lax
@@ -16,7 +18,7 @@
 GROUPS = 4
 G = F // GROUPS
 HALF = F // 2
-UNROLL = 2
+UNROLL = 16
 WAYS = (1, -1)
 
 
@@ -32,24 +34,15 @@
 MESSAGES = len(MESSAGE)
 
 
-def shift_of(here, there):
-    hi = lax.rem(here // 4 + there // 4, 2)
-    dx = lax.rem(here - there + 8, 4)
-    same = 4 - dx + 4 * (dx // 2)
-    other = lax.rem(2 - dx + 8, 8)
-    return hi * other + (1 - hi) * same
-
-
-def chip_at(there, y):
-    dy = lax.rem(y - there + 8, 8)
-    hi = 1 - lax.rem(dy + 1, 8) // 4
-    dx = lax.rem(hi * 2 + (1 - hi) * 4 - dy + 8, 4)
-    return lax.rem(there // 4 + hi, 2) * 4 + lax.rem(there + dx, 4)
+def landing(zl, chip, other):
+    mirrored = lax.rem(chip // 4 + other // 4, 2)
+    return mirrored * (ZS - 1 - zl) + (1 - mirrored) * zl
 
 
 def kernel(
     spectra, flags, mask, weight, observed, out,
     spec_v, flag_v, mask_v, weight_v, obs_v, turn, mine, first, second,
+    scale_t, obs_t, rows_v, res_t,
     gf_own, gf_got, gf_sum, gf_in, gh_own, gh_in, gs_own, gs_got, gz_own, gz_in,
     load_sem, put_s, put_r, zs_s, zs_r, hi_s, hi_r, x_s, x_r, pair_s, pair_r, ring_s, ring_r,
     gp_s, gp_r, gx_s, gx_r, gh_s, gh_r, red_s, red_r, z_s, z_r,
@@ -98,19 +91,31 @@
     barrier = pltpu.get_barrier_semaphore()
     partner = device(y, zl, chip, 1 - core)
     far = lax.rem(hi + 1, 2) * 4 + x
-    giver = chip_at(chip, y)
-    holder = zl // 2 == core
+    own = lax.rem(y, 4)
+    held = landing(zl, chip, 2 * own)
+    holder = held // 2 == core
+    stays = jnp.logical_and(jnp.logical_and(chip == y, chip // 2 == own), zl // 2 == core)
+    my_piece = lax.rem(chip, 2) * 2 + core
+
+    def unless_stays(is_it, body):
+        pl.when(jnp.logical_not(jnp.logical_and(stays, is_it)))(body)
+
+    block_chips = [lax.rem(chip + n, CHIPS) for n in (4, 5, 3, 6, 2, 7, 1)]
     row_chips = [device(y, zl, hi * 4 + lax.rem(x + n, 4), core) for n in range(1, 4)]
     z_line = [device(y, lax.rem(zl + n, ZS), chip, core) for n in range(1, ZS)]
-    peers = [partner, device(y, zl, far, core)] + row_chips + z_line
+    peers = [partner] + [device(y, zl, to, core) for to in block_chips] + z_line
     peers += [device(step_y(way), zl, chip, core) for way in WAYS]
     for peer in peers:
         pl.semaphore_signal(barrier, inc=1, device_id=peer, device_id_type=MESH)
 
     @pl.when(holder)
     def _():
-        for c in range(2):
-            pl.semaphore_signal(barrier, inc=1, device_id=device(chip, zl, giver, c), device_id_type=MESH)
+        for n in range(4):
+
+            @functools.partial(unless_stays, my_piece == n)
+            def _():
+                giver = device(chip, held, 2 * own + n // 2, n % 2)
+                pl.semaphore_signal(barrier, inc=1, device_id=giver, device_id_type=MESH)
 
     for load in loads[2:]:
         load.start()
@@ -131,61 +136,77 @@
             for f in range(F):
                 first[chip, f, 8 * c : 8 * c + 8, :] = pieces[f]
 
-    pl.semaphore_wait(barrier, len(peers) + 1)
-
-    to = device(lax.rem(y + shift_of(chip, y), YS), zl, y, zl // 2)
-    send(mine, second.at[chip, :, lax.rem(zl, 2), eight(core), :], put_s, put_r.at[core], to)
+            @pl.when(stays)
+            def _():
+                for f in range(F):
+                    second[chip, f, lax.rem(zl, 2), 8 * c : 8 * c + 8, :] = pieces[f]
+
+    @pl.when(stays)
+    def _():
+        pl.semaphore_wait(barrier, len(peers) + 1)
+
+    @functools.partial(unless_stays, True)
+    def _():
+        pl.semaphore_wait(barrier, len(peers) + 2)
+
+
+    def put(g, n):
+        to = device(chip // 2 + 4 * n, landing(zl, chip, y), y, zl // 2)
+        dst = second.at[chip, group(g), lax.rem(zl, 2), eight(core), :]
+        return remote(mine.at[group(g)], dst, put_s.at[g * 2 + n], put_r.at[g * 4 + my_piece], to)
+
+    for n in range(2):
+
+        @functools.partial(unless_stays, y // 4 == n)
+        def _():
+            for g in range(GROUPS):
+                put(g, n).start()
 
     send(mine, first.at[chip, :, eight(core), :], hi_s, hi_r, device(y, zl, far, core))
     for n in range(3):
         send(mine, first.at[chip, :, eight(core), :], x_s.at[n], x_r.at[n], row_chips[n])
 
+    for load in loads[2:]:
+        load.wait()
+
+    def over(first_f, last_f, body):
+        def several(n, carry):
+            for m in range(min(UNROLL, last_f - first_f)):
+                body(first_f + n * min(UNROLL, last_f - first_f) + m)
+            return carry
+
+        lax.fori_loop(0, (last_f - first_f) // min(UNROLL, last_f - first_f), several, 0)
+
+    def prepare(f):
+        scale = mask_v[...].astype(F32).astype(BF) * weight_v[f]
+        scale_t[f] = scale.T.reshape(2, 4, 32, 128)
+        for c in range(2):
+            obs_t[f, c] = obs_v[c, f].T.reshape(2, 4, 32, 128)
+
+    over(0, HALF, prepare)
+
     def spread_copies(g):
-        block = second.at[giver, group(g), lax.rem(zl, 2)]
+        block = second.at[pl.ds(2 * own, 2), group(g), lax.rem(held, 2)]
         return [
-            remote(block, block, zs_s.at[g * 3 + n], zs_r.at[g * 2 + lax.rem(zl, 2)], z_line[n]) for n in range(3)
+            remote(block, block, zs_s.at[g * 3 + n], zs_r.at[g * 2 + lax.rem(held, 2)], z_line[n]) for n in range(3)
         ]
 
-    @pl.when(holder)
-    def _():
-        for c in range(2):
-            remote(
-                mine, second.at[giver, :, lax.rem(zl, 2), 8 * c : 8 * c + 8, :], put_s, put_r.at[c], partner
-            ).wait_recv()
-        for g in range(GROUPS):
+    def spread(g):
+        @pl.when(holder)
+        def _():
+            for n in range(4):
+
+                @functools.partial(unless_stays, my_piece == n)
+                def _():
+                    c = n % 2
+                    block = second.at[2 * own + n // 2, group(g), lax.rem(held, 2), 8 * c : 8 * c + 8, :]
+                    remote(mine.at[group(g)], block, put_s.at[0], put_r.at[g * 4 + n], partner).wait_recv()
+
             for copy in spread_copies(g):
                 copy.start()
 
-    def spread_arrival(g, b):
-        block = second.at[giver, group(g), b]
-        remote(block, block, zs_s.at[0], zs_r.at[g * 2 + b], partner).wait_recv()
-
-    def ring_copy(g, w, t, arrival=0):
-        way = WAYS[w]
-        block = second.at[chip_at(chip, step_y(-way * (t - 1 + arrival))), group(g)]
-        n = MESSAGE[g, w, t]
-        return (block, block, ring_s.at[n], ring_r.at[n], device(step_y(way), zl, chip, core))
-
-    def ring_step(t):
-        for g in range(GROUPS):
-            for w in range(2):
-                if t <= steps_of(g, w):
-                    remote(*ring_copy(g, w, t - 1, 1)).wait_recv()
-                    send(*ring_copy(g, w, t))
-
-    for g in range(GROUPS):
-
-        @pl.when(holder)
-        def _():
-            spread_arrival(g, 1 - lax.rem(zl, 2))
-
-        @pl.when(jnp.logical_not(holder))
-        def _():
-            spread_arrival(g, 0)
-            spread_arrival(g, 1)
-
-        for w in range(2):
-            send(*ring_copy(g, w, 1))
+    spread(0)
+    spread(1)
 
     block = first.at[far, :, eight(core), :]
     remote(mine, block, hi_s, hi_r, partner).wait_recv()
@@ -202,49 +223,94 @@
         block = first.at[pl.ds(z_hi * 4, 4), :, eight(core), :]
         send(block, block, pair_s.at[n], pair_r.at[n], partner)
 
-    ring_step(2)
+    over(HALF, F, prepare)
     to_partner(0)
-    ring_step(3)
-    to_partner(1)
-    ring_step(4)
-    for n in range(2):
-        z_hi = hi if n == 0 else lax.rem(hi + 1, 2)
-        block = first.at[pl.ds(z_hi * 4, 4), :, eight(1 - core), :]
-        remote(block, block, pair_s.at[n], pair_r.at[n], partner).wait_recv()
-    for load in loads[2:]:
-        load.wait()
+
+    def spread_arrival(g, b):
+        block = second.at[pl.ds(2 * own, 2), group(g), b]
+        remote(block, block, zs_s.at[0], zs_r.at[g * 2 + b], partner).wait_recv()
+
+    def ring_copy(g, w, t, arrival=0):
+        way = WAYS[w]
+        m = lax.rem(step_y(-way * (t - 1 + arrival)), 4)
+        block = second.at[pl.ds(2 * m, 2), group(g)] if t == 1 else second.at[2 * m + w, group(g)]
+        n = (g * 2 + w) * 2 + t - 1
+        return (block, block, ring_s.at[n], ring_r.at[n], device(step_y(way), zl, chip, core))
+
+    def ring_second():
+        for g in range(GROUPS):
+            for w in range(2):
+                remote(*ring_copy(g, w, 1, 1)).wait_recv()
+                send(*ring_copy(g, w, 2))
+
+    def ring_end():
+        for g in range(GROUPS):
+            for w in range(2):
+                remote(*ring_copy(g, w, 2, 1)).wait_recv()
+
+    def ring_first(g):
+        @pl.when(holder)
+        def _():
+            spread_arrival(g, 1 - lax.rem(held, 2))
+
+        @pl.when(jnp.logical_not(holder))
+        def _():
+            spread_arrival(g, 0)
+            spread_arrival(g, 1)
+
+        for w in range(2):
+            send(*ring_copy(g, w, 1))
+
+    spread(2)
+    ring_first(0)
+    spread(3)
+    for g in range(1, GROUPS):
+        ring_first(g)
 
     lane = lax.broadcasted_iota(jnp.int32, (1, K), 1)
     sign = jnp.where(lane < K // 2, 1.0, -1.0).astype(F32)
 
-    def one_frequency(f):
+    def build_rows(f):
         v = first[:, f].reshape(128, K)
-        turned = (pltpu.roll(v.astype(F32), K // 2, 1) * sign).astype(BF)
-        rows = jnp.concatenate([v, turned], axis=0)
+        rows_v[f, 0] = v
+        rows_v[f, 1] = (pltpu.roll(v.astype(F32), K // 2, 1) * sign).astype(BF)
+
+    def compute(pairs):
+        def one(f):
+            rows = rows_v[f].reshape(256, K)
+            cols = jnp.concatenate(
+                [second[pl.ds(2 * m, 2), f, b].reshape(32, K) for m in pairs for b in range(2)], axis=0
+            )
+            twice = 1 if len(pairs) > 1 else 2
+            cols = jnp.concatenate([cols] * twice, axis=0)
+            cross = lax.dot_general(cols, rows, (((1,), (1,)), ((), ())), preferred_element_type=F32)
+            blocks = []
+            for n, m in enumerate(pairs):
+                for b in range(2):
+                    at = (2 * n + b) * 32
+                    scale = scale_t[f, b, m].astype(F32)
+                    block = [
+                        (scale * (cross[at : at + 32, 128 * c : 128 * c + 128] - obs_t[f, c, b, m].astype(F32))).astype(BF)
+                        for c in range(2)
+                    ]
+                    blocks.append(jnp.concatenate(block, axis=1))
+                    res_t[f, b, m] = blocks[-1]
+            gs = jnp.dot(jnp.concatenate(blocks * twice, axis=0), rows, preferred_element_type=F32)
+            for n, m in enumerate(pairs):
+                for b in range(2):
+                    at = (2 * n + b) * 32
+                    gs_own[4 * b + m, f] = gs[at : at + 32].astype(BF)
+
+        over(0, F, one)
+
+    def first_gradient(f):
+        residual = res_t[f].reshape(256, 256)
         cols = jnp.concatenate([second[:, f, b].reshape(128, K) for b in range(2)], axis=0)
-        cross = lax.dot_general(rows, cols, (((1,), (1,)), ((), ())), preferred_element_type=F32)
-        scale = mask_v[...].astype(F32) * weight_v[f].astype(F32)
-        residual = jnp.concatenate(
-            [(scale * (cross[128 * c : 128 * c + 128] - obs_v[c, f].astype(F32))).astype(BF) for c in range(2)], axis=0
-        )
-        prod = jnp.dot(residual, cols, preferred_element_type=F32)
+        prod = lax.dot_general(residual, cols, (((0,), (0,)), ((), ())), preferred_element_type=F32)
         gf = prod[:128] - pltpu.roll(prod[128:], K // 2, 1) * sign
         gf = gf.reshape(CHIPS, 2, 8, K)
         for c in range(2):
             gf_own[c, :, f] = gf[:, c].astype(BF)
-        gs = lax.dot_general(residual, rows, (((0,), (0,)), ((), ())), preferred_element_type=F32)
-        gs_own[:, f] = gs.reshape(YS, 32, K).astype(BF)
-
-    def compute(g):
-        for w in range(2):
-            remote(*ring_copy(g, w, steps_of(g, w), 1)).wait_recv()
-
-        def pair_of(n, carry):
-            for m in range(UNROLL):
-                one_frequency(g * G + n * UNROLL + m)
-            return carry
-
-        lax.fori_loop(0, G // UNROLL, pair_of, 0)
 
     def red_copy(g, w, t):
         way = WAYS[w]
@@ -252,16 +318,17 @@
         src = gs_own.at[step_y(way * (steps_of(g, w) - t + 1)), group(g)]
         return (src, gs_got.at[n], red_s.at[n], red_r.at[n], device(step_y(way), zl, chip, core))
 
-    def reduce(g, t):
-        for w in range(2):
-            steps = steps_of(g, w)
-            if t > steps:
-                continue
-            if t > 1:
-                remote(*red_copy(g, w, t - 1)).wait_recv()
-                acc = gs_own.at[step_y(WAYS[w] * (steps - t + 1)), group(g)]
-                acc[...] = (acc[...].astype(F32) + gs_got[MESSAGE[g, w, t - 1]].astype(F32)).astype(BF)
-            send(*red_copy(g, w, t))
+    def reduce(distance, start=0, stop=GROUPS):
+        for g in range(start, stop):
+            for w in range(2):
+                t = steps_of(g, w) - distance + 1
+                if t < 1:
+                    continue
+                if t > 1:
+                    remote(*red_copy(g, w, t - 1)).wait_recv()
+                    acc = gs_own.at[step_y(WAYS[w] * distance), group(g)]
+                    acc[...] = (acc[...].astype(F32) + gs_got[MESSAGE[g, w, t - 1]].astype(F32)).astype(BF)
+                send(*red_copy(g, w, t))
 
     def reduced(g):
         total = gs_own[y, group(g)].astype(F32)
@@ -305,34 +372,34 @@
         gh_own[:, half(n)] = value.astype(BF)
         send(*gf_hi(n))
 
-    compute(0)
-    reduce(0, 1)
-    compute(1)
-    reduce(1, 1)
+    to_partner(1)
+    for n in range(2):
+        z_hi = hi if n == 0 else lax.rem(hi + 1, 2)
+        block = first.at[pl.ds(z_hi * 4, 4), :, eight(1 - core), :]
+        remote(block, block, pair_s.at[n], pair_r.at[n], partner).wait_recv()
+    over(0, F, build_rows)
+    compute([own])
+    reduce(4)
+    ring_second()
+    compute([lax.rem(y + 1, 4), lax.rem(y + 3, 4)])
+    reduce(3)
+    ring_end()
+    compute([lax.rem(y + 2, 4)])
+    over(0, HALF, first_gradient)
     send(*gf_pair(0))
-    compute(2)
-    reduce(2, 1)
-    reduce(0, 2)
+    reduce(2)
+    over(HALF, F, first_gradient)
+    send(*gf_pair(1))
     gf_along_x(0)
-    compute(3)
-    reduce(3, 1)
-    send(*gf_pair(1))
-    reduce(1, 2)
-    reduce(2, 2)
-    reduce(0, 3)
+    reduce(1, 0, 2)
     gf_along_x(1)
-    reduce(3, 2)
-    reduce(1, 3)
+    reduce(1, 2, 4)
     gf_across(0)
-    reduce(2, 3)
-    reduce(0, 4)
-    reduce(3, 3)
-    reduce(1, 4)
+    reduced(0)
+    reduced(1)
     gf_across(1)
-    reduce(2, 4)
-    reduce(3, 4)
-    for g in range(GROUPS):
-        reduced(g)
+    reduced(2)
+    reduced(3)
 
     def put_out(value, out):
         turn[...] = value.reshape(8 * F, K)
@@ -352,6 +419,13 @@
 
     for copy in sent:
         copy.wait_send()
+    for n in range(2):
+
+        @functools.partial(unless_stays, y // 4 == n)
+        def _():
+            for g in range(GROUPS):
+                put(g, n).wait_send()
+
 
     @pl.when(holder)
     def _():
@@ -383,6 +457,10 @@
             vmem((F, 8, K), BF),
             vmem((CHIPS, F, 16, K), BF),
             vmem((CHIPS, F, 2, 16, K), BF),
+            vmem((F, 2, 4, 32, 128), BF),
+            vmem((F, 2, 2, 4, 32, 128), BF),
+            vmem((F, 2, 128, K), BF),
+            vmem((F, 2, 4, 32, 256), BF),
             vmem((2, CHIPS, F, 8, K), BF),
             vmem((CHIPS, F, 8, K), BF),
             vmem((2, 4, F, 8, K), BF),
@@ -394,12 +472,12 @@
             vmem((ZS, F, 8, K), BF),
             vmem((ZS - 1, F, 8, K), BF),
             dma((5,)),
-            dma, dma((2,)),
+            dma((2 * GROUPS,)), dma((4 * GROUPS,)),
             dma((3 * GROUPS,)), dma((2 * GROUPS,)),
             dma, dma,
             dma((6,)), dma((6,)),
             dma((2,)), dma((2,)),
-            dma((MESSAGES,)), dma((MESSAGES,)),
+            dma((4 * GROUPS,)), dma((4 * GROUPS,)),
             dma((2,)), dma((2,)),
             dma((6,)), dma((6,)),
             dma((2,)), dma((2,)),

time: 62.7 us -> 60.7 us (0.968)
  the two profiles are of different devices: /device:TPU:6 before, /device:TPU:1 now
where the time goes in v3:
time: 60.7 us; the launch traced here: 60.5 us
  Pallas kernels  59.9 us (99%)
  between operations  0.64 us (1%)
    pallas_call x1, Pallas kernels, per_device(): pl.pallas_call(kernel, out_shape=jax.ShapeDtypeStruct((2, 8, F, K), BF),...  58.4 us
    pallas_call x1, Pallas kernels, per_device(): pl.pallas_call(finish, out_shape=(jax.ShapeDtypeStruct((8, F, K), BF), ja...  1.47 us

profile of v3, /device:TPU:1, one launch (start us, length us, event | category | flops | bytes accessed | tf_op | source)
XLA Modules:
  0.0 60.5 jit_solution(14809893832671851270)
XLA Ops:
  0.6 58.4 %shard_map.68.both = bf16[2,8,16,128]{3,2,1,0:T(8,128)(2,1)} custom-call(bf16[8,16,128]{2,1,0:T(8,128)(2,1)} %spectra.1, s32[8,64]{1,0:T(8,128)} %flags.1, s32[128,256]{1,0:T(8,128)} %mask.1, bf16[16,128,256]{2,1,0:T(8,128)(2,1)} %weight.1, bf16[2,16,128,256]{3,2,1,0:T(8,128)(2,1)} %observed.1), custom_call_target="tpu_custom_call" | custom-call | tf_op jit(solution)/shard_map/pallas_call | solution.py:445
  59.1 1.5 %shard_map.69 = (bf16[8,16,128]{2,1,0:T(8,128)(2,1)}, bf16[1,8,16,128]{3,2,1,0:T(8,128)(2,1)}) custom-call(bf16[2,8,16,128]{3,2,1,0:T(8,128)(2,1)} %shard_map.68.both), custom_call_target="tpu_custom_call" | custom-call | tf_op jit(solution)/shard_map/pallas_call | solution.py:489

commit v4 on v3

--- a/solution.py
+++ b/solution.py
@@ -15,7 +15,7 @@
 CHIPS = 8
 YS = 8
 ZS = 4
-GROUPS = 4
+GROUPS = 2
 G = F // GROUPS
 HALF = F // 2
 UNROLL = 16
@@ -183,7 +183,7 @@
         for c in range(2):
             obs_t[f, c] = obs_v[c, f].T.reshape(2, 4, 32, 128)
 
-    over(0, HALF, prepare)
+    over(0, F, prepare)
 
     def spread_copies(g):
         block = second.at[pl.ds(2 * own, 2), group(g), lax.rem(held, 2)]
@@ -205,13 +205,6 @@
             for copy in spread_copies(g):
                 copy.start()
 
-    spread(0)
-    spread(1)
-
-    block = first.at[far, :, eight(core), :]
-    remote(mine, block, hi_s, hi_r, partner).wait_recv()
-    for n in range(3):
-        send(block, block, x_s.at[n + 3], x_r.at[n + 3], row_chips[n])
 
     def to_partner(n):
         z_hi = hi if n == 0 else lax.rem(hi + 1, 2)
@@ -223,8 +216,6 @@
         block = first.at[pl.ds(z_hi * 4, 4), :, eight(core), :]
         send(block, block, pair_s.at[n], pair_r.at[n], partner)
 
-    over(HALF, F, prepare)
-    to_partner(0)
 
     def spread_arrival(g, b):
         block = second.at[pl.ds(2 * own, 2), group(g), b]
@@ -261,11 +252,17 @@
         for w in range(2):
             send(*ring_copy(g, w, 1))
 
-    spread(2)
+    spread(0)
+    spread(1)
+    block = first.at[far, :, eight(core), :]
+    remote(mine, block, hi_s, hi_r, partner).wait_recv()
+    for n in range(3):
+        send(block, block, x_s.at[n + 3], x_r.at[n + 3], row_chips[n])
+
     ring_first(0)
-    spread(3)
-    for g in range(1, GROUPS):
-        ring_first(g)
+    to_partner(0)
+    ring_first(1)
+    to_partner(1)
 
     lane = lax.broadcasted_iota(jnp.int32, (1, K), 1)
     sign = jnp.where(lane < K // 2, 1.0, -1.0).astype(F32)
@@ -372,7 +369,6 @@
         gh_own[:, half(n)] = value.astype(BF)
         send(*gf_hi(n))
 
-    to_partner(1)
     for n in range(2):
         z_hi = hi if n == 0 else lax.rem(hi + 1, 2)
         block = first.at[pl.ds(z_hi * 4, 4), :, eight(1 - core), :]
@@ -391,15 +387,13 @@
     over(HALF, F, first_gradient)
     send(*gf_pair(1))
     gf_along_x(0)
-    reduce(1, 0, 2)
+    reduce(1, 0, 1)
     gf_along_x(1)
-    reduce(1, 2, 4)
+    reduce(1, 1, 2)
     gf_across(0)
     reduced(0)
+    gf_across(1)
     reduced(1)
-    gf_across(1)
-    reduced(2)
-    reduced(3)
 
     def put_out(value, out):
         turn[...] = value.reshape(8 * F, K)

time: 60.7 us -> 59.6 us (0.982)
  the two profiles are of different devices: /device:TPU:1 before, /device:TPU:6 now
where the time goes in v4:
time: 59.6 us; the launch traced here: 58.9 us
  Pallas kernels  58.3 us (98%)
  between operations  0.64 us (1%)
    pallas_call x1, Pallas kernels, per_device(): pl.pallas_call(kernel, out_shape=jax.ShapeDtypeStruct((2, 8, F, K), BF),...  56.8 us
    pallas_call x1, Pallas kernels, per_device(): pl.pallas_call(finish, out_shape=(jax.ShapeDtypeStruct((8, F, K), BF), ja...  1.47 us

profile of v4, /device:TPU:6, one launch (start us, length us, event | category | flops | bytes accessed | tf_op | source)
XLA Modules:
  0.0 58.9 jit_solution(16760922233708190142)
XLA Ops:
  0.6 56.8 %shard_map.68.both = bf16[2,8,16,128]{3,2,1,0:T(8,128)(2,1)} custom-call(bf16[8,16,128]{2,1,0:T(8,128)(2,1)} %spectra.1, s32[8,64]{1,0:T(8,128)} %flags.1, s32[128,256]{1,0:T(8,128)} %mask.1, bf16[16,128,256]{2,1,0:T(8,128)(2,1)} %weight.1, bf16[2,16,128,256]{3,2,1,0:T(8,128)(2,1)} %observed.1), custom_call_target="tpu_custom_call" | custom-call | tf_op jit(solution)/shard_map/pallas_call | solution.py:439
  57.5 1.5 %shard_map.69 = (bf16[8,16,128]{2,1,0:T(8,128)(2,1)}, bf16[1,8,16,128]{3,2,1,0:T(8,128)(2,1)}) custom-call(bf16[2,8,16,128]{3,2,1,0:T(8,128)(2,1)} %shard_map.68.both), custom_call_target="tpu_custom_call" | custom-call | tf_op jit(solution)/shard_map/pallas_call | solution.py:483

commit v5 on v4

--- a/solution.py
+++ b/solution.py
@@ -155,11 +155,11 @@
         dst = second.at[chip, group(g), lax.rem(zl, 2), eight(core), :]
         return remote(mine.at[group(g)], dst, put_s.at[g * 2 + n], put_r.at[g * 4 + my_piece], to)
 
-    for n in range(2):
-
-        @functools.partial(unless_stays, y // 4 == n)
-        def _():
-            for g in range(GROUPS):
+    for g in range(GROUPS):
+        for n in range(2):
+
+            @functools.partial(unless_stays, y // 4 == n)
+            def _():
                 put(g, n).start()
 
     send(mine, first.at[chip, :, eight(core), :], hi_s, hi_r, device(y, zl, far, core))
@@ -381,9 +381,9 @@
     reduce(3)
     ring_end()
     compute([lax.rem(y + 2, 4)])
+    reduce(2)
     over(0, HALF, first_gradient)
     send(*gf_pair(0))
-    reduce(2)
     over(HALF, F, first_gradient)
     send(*gf_pair(1))
     gf_along_x(0)

time: 59.6 us -> 60.2 us (1.010)
  Pallas kernels: 58.3 us -> 59 us
    pallas_call x1, Pallas kernels: 56.8 us -> 57.6 us  [per_device(): pl.pallas_call(kernel, out_shape=jax.ShapeDtypeStruct((2, 8, F, K), BF),...]
where the time goes in v5:
time: 60.2 us; the launch traced here: 59.7 us
  Pallas kernels  59 us (98%)
  between operations  0.64 us (1%)
    pallas_call x1, Pallas kernels, per_device(): pl.pallas_call(kernel, out_shape=jax.ShapeDtypeStruct((2, 8, F, K), BF),...  57.6 us
    pallas_call x1, Pallas kernels, per_device(): pl.pallas_call(finish, out_shape=(jax.ShapeDtypeStruct((8, F, K), BF), ja...  1.47 us

profile of v5, /device:TPU:6, one launch (start us, length us, event | category | flops | bytes accessed | tf_op | source)
XLA Modules:
  0.0 59.7 jit_solution(8958132707825639841)
XLA Ops:
  0.6 57.6 %shard_map.68.both = bf16[2,8,16,128]{3,2,1,0:T(8,128)(2,1)} custom-call(bf16[8,16,128]{2,1,0:T(8,128)(2,1)} %spectra.1, s32[8,64]{1,0:T(8,128)} %flags.1, s32[128,256]{1,0:T(8,128)} %mask.1, bf16[16,128,256]{2,1,0:T(8,128)(2,1)} %weight.1, bf16[2,16,128,256]{3,2,1,0:T(8,128)(2,1)} %observed.1), custom_call_target="tpu_custom_call" | custom-call | tf_op jit(solution)/shard_map/pallas_call | solution.py:439
  58.2 1.5 %shard_map.69 = (bf16[8,16,128]{2,1,0:T(8,128)(2,1)}, bf16[1,8,16,128]{3,2,1,0:T(8,128)(2,1)}) custom-call(bf16[2,8,16,128]{3,2,1,0:T(8,128)(2,1)} %shard_map.68.both), custom_call_target="tpu_custom_call" | custom-call | tf_op jit(solution)/shard_map/pallas_call | solution.py:483
